TPU v7x, 32 devices: a whole 2x2x4 slice. The times are simulated.
32 devices in a mesh: lat: 8 (over z, x), lon: 4 (over y, core).
Axes of the slice: x: 2, y: 2, z: 4, core: 2. Of those that a mesh axis runs over, the one named last changes fastest.
Arguments:
- increment: bfloat16 [16, 8, 144, 128], P('lat', 'lon'), may hold values from -6 to 6
- cotangent: bfloat16 [8, 4, 40, 144, 128], P('lat', 'lon'), may hold values from -6 to 6
- weights: bfloat16 [8, 4, 40, 16, 128, 128], P('lat', 'lon'), may hold values from -0.1875 to 0.1875
- source_ids: int32 [8, 4, 40, 16], P('lat', 'lon'), may hold values from 0 to 127, as said below
- counts: int32 [8, 4, 40], P('lat', 'lon'), may hold values from 0 to 16, as said below
Outputs:
- ocean: bfloat16 [8, 4, 40, 144, 128], P('lat', 'lon')
- atmos_adjoint: bfloat16 [16, 8, 144, 128], P('lat', 'lon')
Inputs may be any that keep to these rules, and one draw needn't show every extreme that they name: source_ids[i, j, t, k] = a * 8 + b with block row a between i * 2 - 1 and (i + 1) * 2, and block column b equal, modulo 8, to one of j * 2 - 1 to (j + 1) * 2. `counts`: every device's tile (i, j) has some target block with exactly 16 live slots.
All inputs are finite; a program needn't handle non-finite values.
Results may differ from a plain program's by a relative error of at most 0.001.
Values may be sent and summed in bfloat16 or wider, within the bound.
A program may use at most 192 MiB of HBM per device.

v0:
```python
import functools

import jax
import jax.numpy as jnp
from jax import lax
from jax.experimental import pallas as pl
from jax.experimental.pallas import tpu as pltpu
from jax.sharding import PartitionSpec as P

CHUNK = 16
UNROLL = 8
STEPS = 32767.0
WAYS = ((1, 1), (1, -1), (-1, 1), (-1, -1), (1, 0), (-1, 0), (0, 1), (0, -1))


def away(by, side):
    return [side + 1] if by > 0 else ([0] if by < 0 else list(range(1, side + 1)))


def edge_places(way, side):
    i, j = WAYS[way]
    return [r * (side + 2) + c for r in away(i, side) for c in away(j, side)]


def edge_start(way, side):
    return sum(len(edge_places(w, side)) for w in range(way))


def halo_copies(side):
    copies = []
    for way, (i, j) in enumerate(WAYS):
        sent = [side - 1] if i > 0 else ([0] if i < 0 else list(range(side)))
        held = away(-i, side)
        col = side - 1 if j > 0 else 0
        for r, h in zip(sent, held):
            copies.append((way, r, col, h * (side + 2) + away(-j, side)[0], 1 if j else side))
    return copies


def spread(side, lon_count, ids, counts):
    cycle = side * lon_count
    if cycle & (cycle - 1) == 0:
        row = lax.shift_right_logical(ids, cycle.bit_length() - 1)
        col = ids & (cycle - 1)
    else:
        row = lax.div(ids, cycle)
        col = ids - row * cycle
    ext_row = row - lax.axis_index("lat") * side + 1
    ext_col = col - lax.axis_index("lon") * side + 1
    ext_col = jnp.where(ext_col < 0, ext_col + cycle, ext_col)
    ext_col = jnp.where(ext_col >= cycle, ext_col - cycle, ext_col)
    width = side + 2
    slot = lax.broadcasted_iota(jnp.int32, ids.shape, 0)
    return jnp.where(slot < counts, ext_row * width + ext_col, width * width)


def adjoint_kernel(
    side, lon_count, ids_ref, counts_ref, cot_ref, w_ref, own_ref, code_ref, scale_ref, place_ref,
    acc, cot, w_vmem, ids, counts, live, place, of_target, of_slot, w_sems, sems,
):
    targets, slots = w_ref.shape[2:4]
    cells = w_ref.shape[4]
    width = side + 2
    trash = width * width
    live_copy = pltpu.make_async_copy(counts_ref.at[0], live, sems.at[0])
    counts_copy = pltpu.make_async_copy(counts_ref.at[0], counts, sems.at[1])
    ids_copy = pltpu.make_async_copy(ids_ref.at[0, 0], ids, sems.at[2])
    cot_copy = pltpu.make_async_copy(cot_ref.at[0, 0], cot, sems.at[3])
    live_copy.start()
    counts_copy.start()
    ids_copy.start()
    cot_copy.start()
    live_copy.wait()

    def pairs_of(t):
        return lax.shift_right_logical(live[0, t] + 1, 1)

    def weight_copy(t, at):
        n = pairs_of(t) * 2
        return pltpu.make_async_copy(
            w_ref.at[0, 0, t, pl.ds(0, n)], w_vmem.at[pl.ds(at * 2, n)], w_sems.at[t]
        )

    def issue(t, at):
        n = pairs_of(t)

        @pl.when(n > 0)
        def _():
            weight_copy(t, at).start()

        for j in range(slots // 2):
            of_target[at + j] = t
            of_slot[at + j] = 2 * j
        return at + n

    total = lax.fori_loop(0, targets, issue, 0)
    counts_copy.wait()
    ids_copy.wait()
    place_ref[...] = spread(side, lon_count, ids[...], counts[...])
    place_copy = pltpu.make_async_copy(place_ref, place, sems.at[4])
    place_copy.start()
    acc[...] = jnp.zeros_like(acc)
    cot_copy.wait()
    place_copy.wait()

    def chunk(c, met):
        base = c * CHUNK
        last = of_target[jnp.minimum(base + CHUNK, total) - 1]

        def meet(t, at):
            n = pairs_of(t)

            @pl.when(n > 0)
            def _():
                weight_copy(t, at).wait()

            return at

        lax.fori_loop(met, last + 1, meet, 0)
        for u in range(CHUNK):
            at = base + u
            there = at < total
            t = jnp.where(there, of_target[at], 0)
            k = jnp.where(there, of_slot[at], 0)
            both = lax.dot_general(
                cot[t],
                w_vmem[pl.ds(2 * at, 2)].reshape(2 * cells, cells),
                (((1,), (1,)), ((), ())),
                preferred_element_type=jnp.float32,
            )
            for m in range(2):
                to = jnp.where(there, place[k + m, t], trash)
                acc[to] += both[:, m * cells:(m + 1) * cells]
        return last + 1

    lax.fori_loop(0, lax.div(total + (CHUNK - 1), CHUNK), chunk, 0)
    for r in range(side):
        for c in range(side):
            own_ref[r, c] = acc[(r + 1) * width + c + 1]
    for way in range(len(WAYS)):
        for n, p in enumerate(edge_places(way, side)):
            block = acc[p]
            most = jnp.max(jnp.abs(block), axis=0, keepdims=True)
            steps = jnp.where(most > 0, STEPS / most, 0.0)
            at = edge_start(way, side) + n
            scale_ref[at] = most * (1.0 / STEPS)
            code_ref[at] = jnp.round(block * steps).astype(jnp.int32).astype(jnp.int16)


def exchange_kernel(
    sizes, place_ref, own_ref, part_ref, code_ref, scale_ref, w_ref, ocean_ref, out_ref,
    acc, ext, codes, scales, place, w_vmem, w_sems, sems, halo_send, halo_recv, code_send, code_recv,
    scale_send, scale_recv,
):
    lats, lons = sizes
    lat, lon = lax.axis_index("lat"), lax.axis_index("lon")
    side = out_ref.shape[0]
    width = side + 2
    targets, slots = w_vmem.shape[:2]
    cells = w_vmem.shape[2]
    barrier = pltpu.get_barrier_semaphore()

    def peer(i, j):
        return (lat + i, lax.rem(lon + j + lons, lons))

    def sends(i):
        return (lat + i >= 0) & (lat + i < lats)

    def gets(i):
        return (lat - i >= 0) & (lat - i < lats)

    for i, j in WAYS:
        @pl.when(sends(i))
        def _(i=i, j=j):
            pl.semaphore_signal(
                barrier, inc=1, device_id=peer(i, j), device_id_type=pl.DeviceIdType.MESH
            )

    def weights_of(t):
        return pltpu.make_async_copy(w_ref.at[0, 0, t], w_vmem.at[t], w_sems.at[t])

    place_copy = pltpu.make_async_copy(place_ref, place, sems.at[0])
    place_copy.start()

    @pl.loop(0, targets)
    def _(t):
        weights_of(t).start()

    halos = []
    for n, (way, row, col, to, wide) in enumerate(halo_copies(side)):
        halos.append((WAYS[way][0], pltpu.make_async_remote_copy(
            src_ref=own_ref.at[row, pl.ds(col, wide)],
            dst_ref=ext.at[pl.ds(to, wide)],
            send_sem=halo_send.at[n],
            recv_sem=halo_recv.at[n],
            device_id=peer(*WAYS[way]),
            device_id_type=pl.DeviceIdType.MESH,
        )))
    folds = []
    for way, (i, j) in enumerate(WAYS):
        span = pl.ds(edge_start(way, side), len(edge_places(way, side)))
        for from_ref, to_ref, send, recv in (
            (scale_ref, scales, scale_send, scale_recv), (code_ref, codes, code_send, code_recv)
        ):
            folds.append((i, pltpu.make_async_remote_copy(
                src_ref=from_ref.at[span],
                dst_ref=to_ref.at[span],
                send_sem=send.at[way],
                recv_sem=recv.at[way],
                device_id=peer(i, j),
                device_id_type=pl.DeviceIdType.MESH,
            )))
    north = (lat > 0).astype(jnp.int32)
    south = (lat < lats - 1).astype(jnp.int32)
    pl.semaphore_wait(barrier, 2 + 3 * north + 3 * south)
    for i, copy in halos + folds:
        pl.when(sends(i))(copy.start)
    acc[...] = part_ref[...]
    for r in range(side):
        for c in range(side):
            ext[(r + 1) * width + c + 1] = own_ref[r, c]
    blank = jnp.zeros(ext.shape[1:], ext.dtype)
    ext[width * width] = blank
    for i, row in ((1, 0), (-1, side + 1)):
        @pl.when(jnp.logical_not(gets(i)))
        def _(row=row):
            for c in range(width):
                ext[row * width + c] = blank
    place_copy.wait()
    for i, copy in halos:
        pl.when(gets(i))(copy.wait_recv)

    @pl.loop(0, targets // UNROLL)
    def _(g):
        for u in range(UNROLL):
            weights_of(g * UNROLL + u).wait()
        for u in range(UNROLL):
            t = g * UNROLL + u
            picked = jnp.concatenate([ext[place[k, t]] for k in range(slots)], axis=1)
            blocks = w_vmem[t].reshape(slots * cells, w_vmem.shape[3])
            total = jnp.dot(picked, blocks, preferred_element_type=jnp.float32)
            ocean_ref[0, 0, t] = total.astype(ocean_ref.dtype)

    for i, copy in folds:
        pl.when(gets(i))(copy.wait_recv)
    for way, (i, j) in enumerate(WAYS):
        rows = [r - 1 for r in away(-i, side)] if i == 0 else [0 if i > 0 else side - 1]
        cols = [c - 1 for c in away(-j, side)] if j == 0 else [0 if j > 0 else side - 1]

        @pl.when(gets(i))
        def _(way=way, rows=rows, cols=cols):
            for n, (r, c) in enumerate((r, c) for r in rows for c in cols):
                at = edge_start(way, side) + n
                acc[r, c] += codes[at].astype(jnp.int32).astype(jnp.float32) * scales[at]

    out_ref[...] = acc[...].astype(out_ref.dtype)
    for i, copy in halos + folds:
        pl.when(sends(i))(copy.wait_send)


def body(increment, cotangent, weights, source_ids, counts):
    side, _, levels, cells = increment.shape
    sizes = lax.axis_size("lat"), lax.axis_size("lon")
    vmem = pl.BlockSpec(memory_space=pltpu.VMEM)
    hbm = pl.BlockSpec(memory_space=pltpu.HBM)
    targets, slots = weights.shape[2:4]
    width = side + 2
    flat = (width * width + 1, levels, cells)
    edges = edge_start(len(WAYS), side)
    hops = len(halo_copies(side))
    pairs = targets * slots // 2
    cost = pl.CostEstimate(
        flops=2 * targets * slots * levels * cells * cells,
        bytes_accessed=weights.size * 2,
        transcendentals=0,
    )
    limit = 50 * 1024 * 1024
    own, code, scale, place = pl.pallas_call(
        functools.partial(adjoint_kernel, side, sizes[1]),
        out_shape=[
            jax.ShapeDtypeStruct(increment.shape, jnp.float32),
            jax.ShapeDtypeStruct((edges, levels, cells), jnp.int16),
            jax.ShapeDtypeStruct((edges, 1, cells), jnp.float32),
            jax.ShapeDtypeStruct((slots, targets), jnp.int32),
        ],
        in_specs=[hbm, hbm, hbm, hbm],
        out_specs=[vmem, vmem, vmem, vmem],
        scratch_shapes=[
            pltpu.VMEM(flat, jnp.float32),
            pltpu.VMEM(cotangent.shape[2:], cotangent.dtype),
            pltpu.VMEM((targets * slots + 2 * CHUNK, cells, weights.shape[5]), weights.dtype),
            pltpu.VMEM((slots, targets), jnp.int32),
            pltpu.VMEM((1, targets), jnp.int32),
            pltpu.SMEM((1, targets), jnp.int32),
            pltpu.SMEM((slots, targets), jnp.int32),
            pltpu.SMEM((pairs + CHUNK + slots,), jnp.int32),
            pltpu.SMEM((pairs + CHUNK + slots,), jnp.int32),
            pltpu.SemaphoreType.DMA((targets,)),
            pltpu.SemaphoreType.DMA((5,)),
        ],
        compiler_params=pltpu.CompilerParams(vmem_limit_bytes=limit),
        cost_estimate=cost,
        name="adjoint",
    )(jnp.swapaxes(source_ids, 2, 3), counts, cotangent, weights)
    ways = len(WAYS)
    return pl.pallas_call(
        functools.partial(exchange_kernel, sizes),
        out_shape=[
            jax.ShapeDtypeStruct(cotangent.shape, jnp.bfloat16),
            jax.ShapeDtypeStruct(increment.shape, jnp.bfloat16),
        ],
        in_specs=[vmem, vmem, vmem, vmem, vmem, hbm],
        out_specs=[vmem, vmem],
        scratch_shapes=[
            pltpu.VMEM(increment.shape, jnp.float32),
            pltpu.VMEM(flat, increment.dtype),
            pltpu.VMEM((edges, levels, cells), jnp.int16),
            pltpu.VMEM((edges, 1, cells), jnp.float32),
            pltpu.SMEM((slots, targets), jnp.int32),
            pltpu.VMEM(weights.shape[2:], weights.dtype),
            pltpu.SemaphoreType.DMA((targets,)),
            pltpu.SemaphoreType.DMA((1,)),
        ] + [pltpu.SemaphoreType.DMA((hops,))] * 2 + [pltpu.SemaphoreType.DMA((ways,))] * 4,
        compiler_params=pltpu.CompilerParams(
            collective_id=0, has_side_effects=True, vmem_limit_bytes=limit
        ),
        cost_estimate=cost,
        name="exchange",
    )(place, increment, own, code, scale, weights)


def solution(mesh):
    placed = (
        P("lat", "lon", None, None),
        P("lat", "lon", None, None, None),
        P("lat", "lon", None, None, None, None),
        P("lat", "lon", None, None),
        P("lat", "lon", None),
    )
    return jax.shard_map(
        body,
        mesh=mesh,
        in_specs=placed,
        out_specs=(P("lat", "lon", None, None, None), P("lat", "lon", None, None)),
        check_vma=False,
    )
```

profile of v0, /device:TPU:17, one launch (start us, length us, event | category | flops | bytes accessed | tf_op | source)
XLA Modules:
  0.0 37.6 jit_solution(18296392419359531111)
XLA Ops:
  0.6 0.0 copy-start
  0.6 1.4 %copy-done = bf16[1,1,40,144,128]{4,3,2,1,0:T(8,128)(2,1)S(1)} copy-done((bf16[1,1,40,144,128]{4,3,2,1,0:T(8,128)(2,1)S(1)}, bf16[1,1,40,144,128]{4,3,2,1,0:T(8,128)(2,1)}, u32[]{:S(2)}) %copy-start) | copy-done | bytes 1474584
  2.0 0.0 copy-start.2
  2.0 0.7 %copy-done.2 = s32[1,1,40,16]{2,3,1,0:T(8,128)S(1)} copy-done((s32[1,1,40,16]{2,3,1,0:T(8,128)S(1)}, s32[1,1,40,16]{2,3,1,0:T(8,128)}, u32[]{:S(2)}) %copy-start.2) | copy-done | bytes 2584
  2.7 0.0 copy-start.3
  2.7 0.7 %copy-done.3 = s32[1,1,40]{2,1,0:T(1,128)S(1)} copy-done((s32[1,1,40]{2,1,0:T(1,128)S(1)}, s32[1,1,40]{2,1,0:T(1,128)}, u32[]{:S(2)}) %copy-start.3) | copy-done | bytes 184
  3.4 0.0 copy-start.1
  3.4 9.7 %adjoint.1 = (f32[2,2,144,128]{3,2,1,0:T(8,128)S(1)}, s16[12,144,128]{2,1,0:T(8,128)(2,1)S(1)}, f32[12,1,128]{2,1,0:T(1,128)S(1)}, s32[16,40]{1,0:T(8,128)S(1)}) custom-call(s32[1,1,16,40]{3,2,1,0:T(8,128)S(1)} %bitcast.1, s32[1,1,40]{2,1,0:T(1,128)S(1)} %copy-done.3, bf16[1,1,40,144,128]{4,3,2,1,0:T(8,128)(2,1)S(1)} %copy-done, ...), custom_call_target="tpu_custom_call" | custom-call | flops 3019898880 | bytes 20971520 | tf_op jit(solution)/shard_map/adjoint/pallas_call | solution.py:278
  13.0 0.0 copy-done.1
  13.0 22.8 %exchange.1 = (bf16[1,1,40,144,128]{4,3,2,1,0:T(8,128)(2,1)S(1)}, bf16[2,2,144,128]{3,2,1,0:T(8,128)(2,1)S(1)}) custom-call(s32[16,40]{1,0:T(8,128)S(1)} %get-tuple-element.6.place_ref, bf16[2,2,144,128]{3,2,1,0:T(8,128)(2,1)S(1)} %copy-done.1, f32[2,2,144,128]{3,2,1,0:T(8,128)S(1)} %get-tuple-element.7.part_ref, ...), custom_call_target="tpu_custom_call" | custom-call | flops 3019898880 | bytes 20971520 | tf_op jit(solution)/shard_map/exchange/pallas_call | solution.py:306
  35.8 1.1 %copy.9 = bf16[1,1,40,144,128]{4,3,2,1,0:T(8,128)(2,1)} copy(bf16[1,1,40,144,128]{4,3,2,1,0:T(8,128)(2,1)S(1)} %get-tuple-element.12) | data formatting | bytes 2949120
  36.9 0.7 %copy.10 = bf16[2,2,144,128]{3,2,1,0:T(8,128)(2,1)} copy(bf16[2,2,144,128]{3,2,1,0:T(8,128)(2,1)S(1)} %get-tuple-element.13) | data formatting | bytes 294912
Async XLA Ops:
  0.6 1.4 %copy-start = (bf16[1,1,40,144,128]{4,3,2,1,0:T(8,128)(2,1)S(1)}, bf16[1,1,40,144,128]{4,3,2,1,0:T(8,128)(2,1)}, u32[]{:S(2)}) copy-start(bf16[1,1,40,144,128]{4,3,2,1,0:T(8,128)(2,1)} %cot_ref.1) | copy-start | bytes 4423684
  2.0 0.7 %copy-start.2 = (s32[1,1,40,16]{2,3,1,0:T(8,128)S(1)}, s32[1,1,40,16]{2,3,1,0:T(8,128)}, u32[]{:S(2)}) copy-start(s32[1,1,40,16]{2,3,1,0:T(8,128)} %param.8) | copy-start | bytes 7684
  2.7 0.7 %copy-start.3 = (s32[1,1,40]{2,1,0:T(1,128)S(1)}, s32[1,1,40]{2,1,0:T(1,128)}, u32[]{:S(2)}) copy-start(s32[1,1,40]{2,1,0:T(1,128)} %counts_ref.1) | copy-start | bytes 484
  3.4 9.7 %copy-start.1 = (bf16[2,2,144,128]{3,2,1,0:T(8,128)(2,1)S(1)}, bf16[2,2,144,128]{3,2,1,0:T(8,128)(2,1)}, u32[]{:S(2)}) copy-start(bf16[2,2,144,128]{3,2,1,0:T(8,128)(2,1)} %own_ref.1) | copy-start | bytes 442372
where the time goes:
time: 37.9 us; the launch traced here: 37.6 us
  Pallas kernels  32.4 us (85%)
  local copies, waits for them, and re-layouts  4.49 us (12%)
  between operations  0.67 us (2%)
    pallas_call x1, Pallas kernels, body(): pl.pallas_call(functools.partial(exchange_kernel, sizes), out_shape=[jax....  22.8 us
    pallas_call x1, Pallas kernels, body(): pl.pallas_call(functools.partial(adjoint_kernel, side, sizes[1]), out_sha...  9.66 us
    unnamed x10, local copies, waits for them, and re-layouts  4.49 us

commit v1 on v0

--- a/solution.py
+++ b/solution.py
@@ -7,7 +7,7 @@
 from jax.experimental.pallas import tpu as pltpu
 from jax.sharding import PartitionSpec as P
 
-CHUNK = 16
+CHUNK = 32
 UNROLL = 8
 STEPS = 32767.0
 WAYS = ((1, 1), (1, -1), (-1, 1), (-1, -1), (1, 0), (-1, 0), (0, 1), (0, -1))
@@ -150,7 +150,7 @@
 def exchange_kernel(
     sizes, place_ref, own_ref, part_ref, code_ref, scale_ref, w_ref, ocean_ref, out_ref,
     acc, ext, codes, scales, place, w_vmem, w_sems, sems, halo_send, halo_recv, code_send, code_recv,
-    scale_send, scale_recv,
+    scale_send, scale_recv, relay_send, relay_recv,
 ):
     lats, lons = sizes
     lat, lon = lax.axis_index("lat"), lax.axis_index("lon")
@@ -186,14 +186,32 @@
     def _(t):
         weights_of(t).start()
 
+    def inward(j):
+        return j == 1 - 2 * lax.rem(lon, 2)
+
     halos = []
     for n, (way, row, col, to, wide) in enumerate(halo_copies(side)):
-        halos.append((WAYS[way][0], pltpu.make_async_remote_copy(
+        i, j = WAYS[way]
+        direct = (lambda ok, j=j: ok & jnp.logical_not(inward(j)), lambda ok, j=j: ok & inward(j))
+        send, get = direct if i and j else (lambda ok: ok, lambda ok: ok)
+        halos.append((i, j, send(sends(i)), get(gets(i)), pltpu.make_async_remote_copy(
             src_ref=own_ref.at[row, pl.ds(col, wide)],
             dst_ref=ext.at[pl.ds(to, wide)],
             send_sem=halo_send.at[n],
             recv_sem=halo_recv.at[n],
-            device_id=peer(*WAYS[way]),
+            device_id=peer(i, j),
+            device_id_type=pl.DeviceIdType.MESH,
+        )))
+    odd = lax.rem(lon, 2)
+    relays = []
+    for n, i in enumerate((1, -1)):
+        base = away(-i, side)[0] * width
+        relays.append((i, pltpu.make_async_remote_copy(
+            src_ref=ext.at[pl.ds(base + side - (side - 1) * odd, 1)],
+            dst_ref=ext.at[pl.ds(base + (side + 1) * odd, 1)],
+            send_sem=relay_send.at[n],
+            recv_sem=relay_recv.at[n],
+            device_id=(lat, lon + 1 - 2 * odd),
             device_id_type=pl.DeviceIdType.MESH,
         )))
     folds = []
@@ -213,8 +231,11 @@
     north = (lat > 0).astype(jnp.int32)
     south = (lat < lats - 1).astype(jnp.int32)
     pl.semaphore_wait(barrier, 2 + 3 * north + 3 * south)
-    for i, copy in halos + folds:
-        pl.when(sends(i))(copy.start)
+    halos = [h for h in halos if not h[1]] + [h for h in halos if h[0] and h[1]] + [
+        h for h in halos if not h[0]
+    ]
+    for _, _, send, _, copy in halos:
+        pl.when(send)(copy.start)
     acc[...] = part_ref[...]
     for r in range(side):
         for c in range(side):
@@ -227,8 +248,14 @@
             for c in range(width):
                 ext[row * width + c] = blank
     place_copy.wait()
-    for i, copy in halos:
+    for i, j, _, get, copy in halos:
+        pl.when(get)(copy.wait_recv)
+        if not j:
+            pl.when(get)([copy for at, copy in relays if at == i][0].start)
+    for i, copy in relays:
         pl.when(gets(i))(copy.wait_recv)
+    for i, copy in folds:
+        pl.when(sends(i))(copy.start)
 
     @pl.loop(0, targets // UNROLL)
     def _(g):
@@ -254,7 +281,11 @@
                 acc[r, c] += codes[at].astype(jnp.int32).astype(jnp.float32) * scales[at]
 
     out_ref[...] = acc[...].astype(out_ref.dtype)
-    for i, copy in halos + folds:
+    for _, _, send, _, copy in halos:
+        pl.when(send)(copy.wait_send)
+    for i, copy in relays:
+        pl.when(gets(i))(copy.wait_send)
+    for i, copy in folds:
         pl.when(sends(i))(copy.wait_send)
 
 
@@ -301,7 +332,7 @@
         compiler_params=pltpu.CompilerParams(vmem_limit_bytes=limit),
         cost_estimate=cost,
         name="adjoint",
-    )(jnp.swapaxes(source_ids, 2, 3), counts, cotangent, weights)
+    )(*[pltpu.with_memory_space_constraint(x, pltpu.HBM) for x in (jnp.swapaxes(source_ids, 2, 3), counts, cotangent, weights)])
     ways = len(WAYS)
     return pl.pallas_call(
         functools.partial(exchange_kernel, sizes),
@@ -320,7 +351,8 @@
             pltpu.VMEM(weights.shape[2:], weights.dtype),
             pltpu.SemaphoreType.DMA((targets,)),
             pltpu.SemaphoreType.DMA((1,)),
-        ] + [pltpu.SemaphoreType.DMA((hops,))] * 2 + [pltpu.SemaphoreType.DMA((ways,))] * 4,
+        ] + [pltpu.SemaphoreType.DMA((hops,))] * 2 + [pltpu.SemaphoreType.DMA((ways,))] * 4
+        + [pltpu.SemaphoreType.DMA((2,))] * 2,
         compiler_params=pltpu.CompilerParams(
             collective_id=0, has_side_effects=True, vmem_limit_bytes=limit
         ),

time: 37.9 us -> 30.9 us (0.82)
  Pallas kernels: 32.4 us -> 28.2 us
  local copies, waits for them, and re-layouts: 4.49 us -> 1.78 us
    pallas_call x1, Pallas kernels: 22.8 us -> 19.2 us  [body(): pl.pallas_call(functools.partial(exchange_kernel, sizes), out_shape=[jax....]
    unnamed x10 -> x4, local copies, waits for them, and re-layouts: 4.49 us -> 1.78 us
    pallas_call x1, Pallas kernels: 9.66 us -> 9.02 us  [body(): pl.pallas_call(functools.partial(adjoint_kernel, side, sizes[1]), out_sha...]
where the time goes in v1:
time: 30.9 us; the launch traced here: 30.6 us
  Pallas kernels  28.2 us (91%)
  local copies, waits for them, and re-layouts  1.78 us (6%)
  between operations  0.66 us (2%)
    pallas_call x1, Pallas kernels, body(): pl.pallas_call(functools.partial(exchange_kernel, sizes), out_shape=[jax....  19.2 us
    pallas_call x1, Pallas kernels, body(): pl.pallas_call(functools.partial(adjoint_kernel, side, sizes[1]), out_sha...  9.02 us
    unnamed x4, local copies, waits for them, and re-layouts  1.78 us

profile of v1, /device:TPU:17, one launch (start us, length us, event | category | flops | bytes accessed | tf_op | source)
XLA Modules:
  0.0 30.6 jit_solution(3784310562562121430)
XLA Ops:
  0.6 0.0 copy-start
  0.6 9.0 %adjoint.1 = (f32[2,2,144,128]{3,2,1,0:T(8,128)S(1)}, s16[12,144,128]{2,1,0:T(8,128)(2,1)S(1)}, f32[12,1,128]{2,1,0:T(1,128)S(1)}, s32[16,40]{1,0:T(8,128)S(1)}) custom-call(s32[1,1,16,40]{3,2,1,0:T(8,128)} %bitcast.1, s32[1,1,40]{2,1,0:T(1,128)} %counts_ref.1, bf16[1,1,40,144,128]{4,3,2,1,0:T(8,128)(2,1)} %cot_ref.1, bf16[1,1,40,16,128,128]{5,4,3,2,1,0:T(8,128)(2,1)} %w_ref.3), custom_call_target="tpu_custom_call" | custom-call | flops 3019898880 | bytes 20971520 | tf_op jit(solution)/shard_map/adjoint/pallas_call | solution.py:309
  9.7 0.0 copy-done
  9.7 19.2 %exchange.1 = (bf16[1,1,40,144,128]{4,3,2,1,0:T(8,128)(2,1)S(1)}, bf16[2,2,144,128]{3,2,1,0:T(8,128)(2,1)S(1)}) custom-call(s32[16,40]{1,0:T(8,128)S(1)} %get-tuple-element.6.place_ref, bf16[2,2,144,128]{3,2,1,0:T(8,128)(2,1)S(1)} %copy-done, f32[2,2,144,128]{3,2,1,0:T(8,128)S(1)} %get-tuple-element.7.part_ref, ...), custom_call_target="tpu_custom_call" | custom-call | flops 3019898880 | bytes 20971520 | tf_op jit(solution)/shard_map/exchange/pallas_call | solution.py:337
  28.9 1.1 %copy.9 = bf16[1,1,40,144,128]{4,3,2,1,0:T(8,128)(2,1)} copy(bf16[1,1,40,144,128]{4,3,2,1,0:T(8,128)(2,1)S(1)} %get-tuple-element.12) | data formatting | bytes 2949120
  30.0 0.7 %copy.10 = bf16[2,2,144,128]{3,2,1,0:T(8,128)(2,1)} copy(bf16[2,2,144,128]{3,2,1,0:T(8,128)(2,1)S(1)} %get-tuple-element.13) | data formatting | bytes 294912
Async XLA Ops:
  0.6 9.0 %copy-start = (bf16[2,2,144,128]{3,2,1,0:T(8,128)(2,1)S(1)}, bf16[2,2,144,128]{3,2,1,0:T(8,128)(2,1)}, u32[]{:S(2)}) copy-start(bf16[2,2,144,128]{3,2,1,0:T(8,128)(2,1)} %own_ref.1) | copy-start | bytes 442372

commit v2 on v1

--- a/solution.py
+++ b/solution.py
@@ -8,6 +8,8 @@
 from jax.sharding import PartitionSpec as P
 
 CHUNK = 32
+HEAD = 4
+SHARES = 8
 UNROLL = 8
 STEPS = 32767.0
 WAYS = ((1, 1), (1, -1), (-1, 1), (-1, -1), (1, 0), (-1, 0), (0, 1), (0, -1))
@@ -55,13 +57,12 @@
 
 
 def adjoint_kernel(
-    side, lon_count, ids_ref, counts_ref, cot_ref, w_ref, own_ref, code_ref, scale_ref, place_ref,
-    acc, cot, w_vmem, ids, counts, live, place, of_target, of_slot, w_sems, sems,
+    side, lon_count, ids_ref, counts_ref, cot_ref, w_ref, part_ref, place_ref,
+    cot, w_vmem, ids, counts, live, place, of_target, of_slot, w_sems, sems,
 ):
     targets, slots = w_ref.shape[2:4]
     cells = w_ref.shape[4]
-    width = side + 2
-    trash = width * width
+    trash = part_ref.shape[0] - 1
     live_copy = pltpu.make_async_copy(counts_ref.at[0], live, sems.at[0])
     counts_copy = pltpu.make_async_copy(counts_ref.at[0], counts, sems.at[1])
     ids_copy = pltpu.make_async_copy(ids_ref.at[0, 0], ids, sems.at[2])
@@ -69,88 +70,90 @@
     live_copy.start()
     counts_copy.start()
     ids_copy.start()
+
+    def weight_copy(t, n):
+        return pltpu.make_async_copy(
+            w_ref.at[0, 0, t, pl.ds(0, n)], w_vmem.at[pl.ds(t * slots, n)], w_sems.at[t]
+        )
+
+    for t in range(HEAD):
+        weight_copy(t, slots).start()
     cot_copy.start()
+    part_ref[...] = jnp.zeros_like(part_ref)
     live_copy.wait()
 
     def pairs_of(t):
         return lax.shift_right_logical(live[0, t] + 1, 1)
 
-    def weight_copy(t, at):
-        n = pairs_of(t) * 2
-        return pltpu.make_async_copy(
-            w_ref.at[0, 0, t, pl.ds(0, n)], w_vmem.at[pl.ds(at * 2, n)], w_sems.at[t]
-        )
-
-    def issue(t, at):
-        n = pairs_of(t)
-
-        @pl.when(n > 0)
-        def _():
-            weight_copy(t, at).start()
-
+    def enlist(t, at):
         for j in range(slots // 2):
             of_target[at + j] = t
             of_slot[at + j] = 2 * j
-        return at + n
-
-    total = lax.fori_loop(0, targets, issue, 0)
+        return at + pairs_of(t)
+
+    def issue(t, at):
+        n = pairs_of(t)
+
+        @pl.when(n > 0)
+        def _():
+            weight_copy(t, n * 2).start()
+
+        return enlist(t, at)
+
+    total = lax.fori_loop(HEAD, targets, issue, lax.fori_loop(0, HEAD, enlist, 0))
     counts_copy.wait()
     ids_copy.wait()
     place_ref[...] = spread(side, lon_count, ids[...], counts[...])
     place_copy = pltpu.make_async_copy(place_ref, place, sems.at[4])
     place_copy.start()
-    acc[...] = jnp.zeros_like(acc)
     cot_copy.wait()
     place_copy.wait()
+    for t in range(HEAD):
+        weight_copy(t, slots).wait()
 
     def chunk(c, met):
         base = c * CHUNK
         last = of_target[jnp.minimum(base + CHUNK, total) - 1]
 
-        def meet(t, at):
+        def meet(t, carry):
             n = pairs_of(t)
 
             @pl.when(n > 0)
             def _():
-                weight_copy(t, at).wait()
-
-            return at
+                weight_copy(t, n * 2).wait()
+
+            return carry
 
         lax.fori_loop(met, last + 1, meet, 0)
         for u in range(CHUNK):
-            at = base + u
-            there = at < total
-            t = jnp.where(there, of_target[at], 0)
-            k = jnp.where(there, of_slot[at], 0)
+            there = base + u < total
+            t = jnp.where(there, of_target[base + u], 0)
+            k = jnp.where(there, of_slot[base + u], 0)
             both = lax.dot_general(
                 cot[t],
-                w_vmem[pl.ds(2 * at, 2)].reshape(2 * cells, cells),
+                w_vmem[pl.ds(t * slots + k, 2)].reshape(2 * cells, cells),
                 (((1,), (1,)), ((), ())),
                 preferred_element_type=jnp.float32,
             )
             for m in range(2):
                 to = jnp.where(there, place[k + m, t], trash)
-                acc[to] += both[:, m * cells:(m + 1) * cells]
-        return last + 1
-
-    lax.fori_loop(0, lax.div(total + (CHUNK - 1), CHUNK), chunk, 0)
-    for r in range(side):
-        for c in range(side):
-            own_ref[r, c] = acc[(r + 1) * width + c + 1]
-    for way in range(len(WAYS)):
-        for n, p in enumerate(edge_places(way, side)):
-            block = acc[p]
-            most = jnp.max(jnp.abs(block), axis=0, keepdims=True)
-            steps = jnp.where(most > 0, STEPS / most, 0.0)
-            at = edge_start(way, side) + n
-            scale_ref[at] = most * (1.0 / STEPS)
-            code_ref[at] = jnp.round(block * steps).astype(jnp.int32).astype(jnp.int16)
+                part_ref[to] += both[:, m * cells:(m + 1) * cells]
+        return jnp.maximum(met, last + 1)
+
+    lax.fori_loop(0, lax.div(total + (CHUNK - 1), CHUNK), chunk, HEAD)
+
+
+def encode(block, code_ref, scale_ref, at):
+    most = jnp.max(jnp.abs(block), axis=0, keepdims=True)
+    steps = jnp.where(most > 0, STEPS / most, 0.0)
+    scale_ref[at] = most * (1.0 / STEPS)
+    code_ref[at] = jnp.round(block * steps).astype(jnp.int32).astype(jnp.int16)
 
 
 def exchange_kernel(
-    sizes, place_ref, own_ref, part_ref, code_ref, scale_ref, w_ref, ocean_ref, out_ref,
-    acc, ext, codes, scales, place, w_vmem, w_sems, sems, halo_send, halo_recv, code_send, code_recv,
-    scale_send, scale_recv, relay_send, relay_recv,
+    sizes, place_ref, own_ref, part_ref, w_ref, ocean_ref, out_ref,
+    code_ref, scale_ref, codes, scales, nears, acc, ext, place, w_vmem, w_sems, sems, halo_send, halo_recv, code_send, code_recv,
+    scale_send, scale_recv, relay_send, relay_recv, near_send, near_recv,
 ):
     lats, lons = sizes
     lat, lon = lax.axis_index("lat"), lax.axis_index("lon")
@@ -217,17 +220,36 @@
     folds = []
     for way, (i, j) in enumerate(WAYS):
         span = pl.ds(edge_start(way, side), len(edge_places(way, side)))
-        for from_ref, to_ref, send, recv in (
+        send, get = sends(i), gets(i)
+        if i and j:
+            send, get = send & jnp.logical_not(inward(j)), get & inward(j)
+        for from_ref, to_ref, out, back in (
             (scale_ref, scales, scale_send, scale_recv), (code_ref, codes, code_send, code_recv)
         ):
-            folds.append((i, pltpu.make_async_remote_copy(
+            folds.append((i, j, send, get, pltpu.make_async_remote_copy(
                 src_ref=from_ref.at[span],
                 dst_ref=to_ref.at[span],
-                send_sem=send.at[way],
-                recv_sem=recv.at[way],
+                send_sem=out.at[way],
+                recv_sem=back.at[way],
                 device_id=peer(i, j),
                 device_id_type=pl.DeviceIdType.MESH,
             )))
+    partner = (lat, lon + 1 - 2 * odd)
+    near = []
+    for n, i in enumerate((1, -1)):
+        far = away(i, side)[0] * width + (side + 1) * (1 - odd)
+        near.append((i, pltpu.make_async_remote_copy(
+            src_ref=part_ref.at[pl.ds(far, 1)],
+            dst_ref=nears.at[pl.ds(n, 1)],
+            send_sem=near_send.at[n],
+            recv_sem=near_recv.at[n],
+            device_id=partner,
+            device_id_type=pl.DeviceIdType.MESH,
+        )))
+    for way, (i, j) in enumerate(WAYS):
+        for n, p in enumerate(edge_places(way, side)):
+            if j:
+                encode(part_ref[p], code_ref, scale_ref, edge_start(way, side) + n)
     north = (lat > 0).astype(jnp.int32)
     south = (lat < lats - 1).astype(jnp.int32)
     pl.semaphore_wait(barrier, 2 + 3 * north + 3 * south)
@@ -236,9 +258,11 @@
     ]
     for _, _, send, _, copy in halos:
         pl.when(send)(copy.start)
-    acc[...] = part_ref[...]
+    for i, copy in near:
+        pl.when(sends(i))(copy.start)
     for r in range(side):
         for c in range(side):
+            acc[r, c] = part_ref[(r + 1) * width + c + 1]
             ext[(r + 1) * width + c + 1] = own_ref[r, c]
     blank = jnp.zeros(ext.shape[1:], ext.dtype)
     ext[width * width] = blank
@@ -248,14 +272,24 @@
             for c in range(width):
                 ext[row * width + c] = blank
     place_copy.wait()
+    for n, (i, copy) in enumerate(near):
+        @pl.when(sends(i))
+        def _(n=n, i=i, copy=copy):
+            copy.wait_recv()
+            way = WAYS.index((i, 0))
+            for at, p in enumerate(edge_places(way, side)):
+                meets = (1 - odd) * (side - 1) == at
+                block = part_ref[p] + jnp.where(meets, nears[n], 0.0)
+                encode(block, code_ref, scale_ref, edge_start(way, side) + at)
+
     for i, j, _, get, copy in halos:
         pl.when(get)(copy.wait_recv)
         if not j:
             pl.when(get)([copy for at, copy in relays if at == i][0].start)
     for i, copy in relays:
         pl.when(gets(i))(copy.wait_recv)
-    for i, copy in folds:
-        pl.when(sends(i))(copy.start)
+    for _, _, send, _, copy in folds:
+        pl.when(send)(copy.start)
 
     @pl.loop(0, targets // UNROLL)
     def _(g):
@@ -268,13 +302,13 @@
             total = jnp.dot(picked, blocks, preferred_element_type=jnp.float32)
             ocean_ref[0, 0, t] = total.astype(ocean_ref.dtype)
 
-    for i, copy in folds:
-        pl.when(gets(i))(copy.wait_recv)
+    for _, _, _, get, copy in folds:
+        pl.when(get)(copy.wait_recv)
     for way, (i, j) in enumerate(WAYS):
         rows = [r - 1 for r in away(-i, side)] if i == 0 else [0 if i > 0 else side - 1]
         cols = [c - 1 for c in away(-j, side)] if j == 0 else [0 if j > 0 else side - 1]
 
-        @pl.when(gets(i))
+        @pl.when(gets(i) & inward(j) if i and j else gets(i))
         def _(way=way, rows=rows, cols=cols):
             for n, (r, c) in enumerate((r, c) for r in rows for c in cols):
                 at = edge_start(way, side) + n
@@ -285,8 +319,25 @@
         pl.when(send)(copy.wait_send)
     for i, copy in relays:
         pl.when(gets(i))(copy.wait_send)
-    for i, copy in folds:
+    for i, copy in near:
         pl.when(sends(i))(copy.wait_send)
+    for _, _, send, _, copy in folds:
+        pl.when(send)(copy.wait_send)
+
+
+def deliver_kernel(ocean_ref, part_ref, ocean_out, part_out, sems):
+    targets = ocean_ref.shape[2]
+    step = -(-targets // SHARES)
+    copies = [pltpu.make_async_copy(part_ref, part_out, sems.at[SHARES])]
+    for n in range(SHARES):
+        span = pl.ds(n * step, max(min(step, targets - n * step), 0))
+        copies.append(
+            pltpu.make_async_copy(ocean_ref.at[0, 0, span], ocean_out.at[0, 0, span], sems.at[n])
+        )
+    for copy in copies:
+        copy.start()
+    for copy in copies:
+        copy.wait()
 
 
 def body(increment, cotangent, weights, source_ids, counts):
@@ -306,20 +357,21 @@
         transcendentals=0,
     )
     limit = 50 * 1024 * 1024
-    own, code, scale, place = pl.pallas_call(
+    whole, rows, held_counts = (
+        pltpu.with_memory_space_constraint(x, pltpu.HBM)
+        for x in (weights, jnp.swapaxes(source_ids, 2, 3), counts)
+    )
+    part, place = pl.pallas_call(
         functools.partial(adjoint_kernel, side, sizes[1]),
         out_shape=[
-            jax.ShapeDtypeStruct(increment.shape, jnp.float32),
-            jax.ShapeDtypeStruct((edges, levels, cells), jnp.int16),
-            jax.ShapeDtypeStruct((edges, 1, cells), jnp.float32),
+            jax.ShapeDtypeStruct(flat, jnp.float32),
             jax.ShapeDtypeStruct((slots, targets), jnp.int32),
         ],
         in_specs=[hbm, hbm, hbm, hbm],
-        out_specs=[vmem, vmem, vmem, vmem],
+        out_specs=[vmem, vmem],
         scratch_shapes=[
-            pltpu.VMEM(flat, jnp.float32),
             pltpu.VMEM(cotangent.shape[2:], cotangent.dtype),
-            pltpu.VMEM((targets * slots + 2 * CHUNK, cells, weights.shape[5]), weights.dtype),
+            pltpu.VMEM((targets * slots, cells, weights.shape[5]), weights.dtype),
             pltpu.VMEM((slots, targets), jnp.int32),
             pltpu.VMEM((1, targets), jnp.int32),
             pltpu.SMEM((1, targets), jnp.int32),
@@ -332,33 +384,46 @@
         compiler_params=pltpu.CompilerParams(vmem_limit_bytes=limit),
         cost_estimate=cost,
         name="adjoint",
-    )(*[pltpu.with_memory_space_constraint(x, pltpu.HBM) for x in (jnp.swapaxes(source_ids, 2, 3), counts, cotangent, weights)])
+    )(rows, held_counts, pltpu.with_memory_space_constraint(cotangent, pltpu.HBM), whole)
     ways = len(WAYS)
-    return pl.pallas_call(
+    coded = [
+        pltpu.VMEM((edges, levels, cells), jnp.int16),
+        pltpu.VMEM((edges, 1, cells), jnp.float32),
+    ]
+    results = [
+        jax.ShapeDtypeStruct(cotangent.shape, jnp.bfloat16),
+        jax.ShapeDtypeStruct(increment.shape, jnp.bfloat16),
+    ]
+    ocean, adjoint = pl.pallas_call(
         functools.partial(exchange_kernel, sizes),
-        out_shape=[
-            jax.ShapeDtypeStruct(cotangent.shape, jnp.bfloat16),
-            jax.ShapeDtypeStruct(increment.shape, jnp.bfloat16),
-        ],
-        in_specs=[vmem, vmem, vmem, vmem, vmem, hbm],
+        out_shape=results,
+        in_specs=[vmem, vmem, vmem, hbm],
         out_specs=[vmem, vmem],
-        scratch_shapes=[
+        scratch_shapes=coded + coded + [
+            pltpu.VMEM((2, levels, cells), jnp.float32),
             pltpu.VMEM(increment.shape, jnp.float32),
             pltpu.VMEM(flat, increment.dtype),
-            pltpu.VMEM((edges, levels, cells), jnp.int16),
-            pltpu.VMEM((edges, 1, cells), jnp.float32),
             pltpu.SMEM((slots, targets), jnp.int32),
             pltpu.VMEM(weights.shape[2:], weights.dtype),
             pltpu.SemaphoreType.DMA((targets,)),
             pltpu.SemaphoreType.DMA((1,)),
         ] + [pltpu.SemaphoreType.DMA((hops,))] * 2 + [pltpu.SemaphoreType.DMA((ways,))] * 4
-        + [pltpu.SemaphoreType.DMA((2,))] * 2,
+        + [pltpu.SemaphoreType.DMA((2,))] * 4,
         compiler_params=pltpu.CompilerParams(
             collective_id=0, has_side_effects=True, vmem_limit_bytes=limit
         ),
         cost_estimate=cost,
         name="exchange",
-    )(place, increment, own, code, scale, weights)
+    )(place, increment, part, whole)
+    return pl.pallas_call(
+        deliver_kernel,
+        out_shape=results,
+        in_specs=[vmem] * 2,
+        out_specs=[hbm] * 2,
+        scratch_shapes=[pltpu.SemaphoreType.DMA((SHARES + 1,))],
+        compiler_params=pltpu.CompilerParams(vmem_limit_bytes=limit),
+        name="deliver",
+    )(ocean, adjoint)
 
 
 def solution(mesh):

time: 30.9 us -> 29.1 us (0.942)
  local copies, waits for them, and re-layouts: 1.78 us -> 0.01 us
    unnamed x4 -> x2, local copies, waits for them, and re-layouts: 1.78 us -> 0.01 us
    pallas_call x1 -> x2, Pallas kernels: 19.2 us -> 19.6 us  [the longest x1 18.3 us: body(): pl.pallas_call(functools.partial(exchange_kernel, sizes), out_shape=resul...]
    pallas_call x1, Pallas kernels: 9.02 us -> 8.64 us  [body(): pl.pallas_call(functools.partial(adjoint_kernel, side, sizes[1]), out_sha...]
where the time goes in v2:
time: 29.1 us; the launch traced here: 28.9 us
  Pallas kernels  28.2 us (97%)
  between operations  0.66 us (2%)
    pallas_call x1, Pallas kernels, body(): pl.pallas_call(functools.partial(exchange_kernel, sizes), out_shape=resul...  18.3 us
    pallas_call x1, Pallas kernels, body(): pl.pallas_call(functools.partial(adjoint_kernel, side, sizes[1]), out_sha...  8.64 us
    pallas_call x1, Pallas kernels, body(): pl.pallas_call(deliver_kernel, out_shape=results, in_specs=[vmem] * 2, ou...  1.23 us

profile of v2, /device:TPU:17, one launch (start us, length us, event | category | flops | bytes accessed | tf_op | source)
XLA Modules:
  0.0 28.9 jit_solution(14824458652814813198)
XLA Ops:
  0.6 0.0 copy-start
  0.6 8.6 %adjoint.1 = (f32[17,144,128]{2,1,0:T(8,128)S(1)}, s32[16,40]{1,0:T(8,128)S(1)}) custom-call(s32[1,1,16,40]{3,2,1,0:T(8,128)} %bitcast.1, s32[1,1,40]{2,1,0:T(1,128)} %counts_ref.1, bf16[1,1,40,144,128]{4,3,2,1,0:T(8,128)(2,1)} %cot_ref.1, bf16[1,1,40,16,128,128]{5,4,3,2,1,0:T(8,128)(2,1)} %w_ref.3), custom_call_target="tpu_custom_call" | custom-call | flops 3019898880 | bytes 20971520 | tf_op jit(solution)/shard_map/adjoint/pallas_call | solution.py:364
  9.3 0.0 copy-done
  9.3 18.3 %exchange.1 = (bf16[1,1,40,144,128]{4,3,2,1,0:T(8,128)(2,1)S(1)}, bf16[2,2,144,128]{3,2,1,0:T(8,128)(2,1)S(1)}) custom-call(s32[16,40]{1,0:T(8,128)S(1)} %get-tuple-element.6.place_ref, bf16[2,2,144,128]{3,2,1,0:T(8,128)(2,1)S(1)} %copy-done, f32[17,144,128]{2,1,0:T(8,128)S(1)} %get-tuple-element.7.part_ref, bf16[1,1,40,16,128,128]{5,4,3,2,1,0:T(8,128)(2,1)} %w_ref.3), custom_call_target="tpu_custom_call" | custom-call | flops 3019898880 | bytes 20971520 | tf_op jit(solution)/shard_map/exchange/pallas_call | solution.py:397
  27.6 1.2 %deliver.1 = (bf16[1,1,40,144,128]{4,3,2,1,0:T(8,128)(2,1)}, bf16[2,2,144,128]{3,2,1,0:T(8,128)(2,1)}) custom-call(bf16[1,1,40,144,128]{4,3,2,1,0:T(8,128)(2,1)S(1)} %get-tuple-element.8.ocean_ref, bf16[2,2,144,128]{3,2,1,0:T(8,128)(2,1)S(1)} %get-tuple-element.9.part_ref), custom_call_target="tpu_custom_call" | custom-call | tf_op jit(solution)/shard_map/deliver/pallas_call | solution.py:418
Async XLA Ops:
  0.6 8.7 %copy-start = (bf16[2,2,144,128]{3,2,1,0:T(8,128)(2,1)S(1)}, bf16[2,2,144,128]{3,2,1,0:T(8,128)(2,1)}, u32[]{:S(2)}) copy-start(bf16[2,2,144,128]{3,2,1,0:T(8,128)(2,1)} %own_ref.1) | copy-start | bytes 442372

commit v3 on v2

--- a/solution.py
+++ b/solution.py
@@ -10,7 +10,7 @@
 CHUNK = 32
 HEAD = 4
 SHARES = 8
-UNROLL = 8
+UNROLL = 10
 STEPS = 32767.0
 WAYS = ((1, 1), (1, -1), (-1, 1), (-1, -1), (1, 0), (-1, 0), (0, 1), (0, -1))
 
@@ -246,10 +246,6 @@
             device_id=partner,
             device_id_type=pl.DeviceIdType.MESH,
         )))
-    for way, (i, j) in enumerate(WAYS):
-        for n, p in enumerate(edge_places(way, side)):
-            if j:
-                encode(part_ref[p], code_ref, scale_ref, edge_start(way, side) + n)
     north = (lat > 0).astype(jnp.int32)
     south = (lat < lats - 1).astype(jnp.int32)
     pl.semaphore_wait(barrier, 2 + 3 * north + 3 * south)
@@ -260,6 +256,10 @@
         pl.when(send)(copy.start)
     for i, copy in near:
         pl.when(sends(i))(copy.start)
+    for way, (i, j) in enumerate(WAYS):
+        for n, p in enumerate(edge_places(way, side)):
+            if j:
+                encode(part_ref[p], code_ref, scale_ref, edge_start(way, side) + n)
     for r in range(side):
         for c in range(side):
             acc[r, c] = part_ref[(r + 1) * width + c + 1]

time: 29.1 us -> 29 us (level)
  Pallas kernels: 28.2 us -> 27.9 us
where the time goes in v3:
time: 29 us; the launch traced here: 28.5 us
  Pallas kernels  27.9 us (96%)
  between operations  0.66 us (2%)
    pallas_call x1, Pallas kernels, body(): pl.pallas_call(functools.partial(exchange_kernel, sizes), out_shape=resul...  18.2 us
    pallas_call x1, Pallas kernels, body(): pl.pallas_call(functools.partial(adjoint_kernel, side, sizes[1]), out_sha...  8.48 us
    pallas_call x1, Pallas kernels, body(): pl.pallas_call(deliver_kernel, out_shape=results, in_specs=[vmem] * 2, ou...  1.23 us

profile of v3, /device:TPU:17, one launch (start us, length us, event | category | flops | bytes accessed | tf_op | source)
XLA Modules:
  0.0 28.5 jit_solution(17948436529150905446)
XLA Ops:
  0.6 0.0 copy-start
  0.6 8.5 %adjoint.1 = (f32[17,144,128]{2,1,0:T(8,128)S(1)}, s32[16,40]{1,0:T(8,128)S(1)}) custom-call(s32[1,1,16,40]{3,2,1,0:T(8,128)} %bitcast.1, s32[1,1,40]{2,1,0:T(1,128)} %counts_ref.1, bf16[1,1,40,144,128]{4,3,2,1,0:T(8,128)(2,1)} %cot_ref.1, bf16[1,1,40,16,128,128]{5,4,3,2,1,0:T(8,128)(2,1)} %w_ref.3), custom_call_target="tpu_custom_call" | custom-call | flops 3019898880 | bytes 20971520 | tf_op jit(solution)/shard_map/adjoint/pallas_call | solution.py:364
  9.1 0.0 copy-done
  9.1 18.2 %exchange.1 = (bf16[1,1,40,144,128]{4,3,2,1,0:T(8,128)(2,1)S(1)}, bf16[2,2,144,128]{3,2,1,0:T(8,128)(2,1)S(1)}) custom-call(s32[16,40]{1,0:T(8,128)S(1)} %get-tuple-element.6.place_ref, bf16[2,2,144,128]{3,2,1,0:T(8,128)(2,1)S(1)} %copy-done, f32[17,144,128]{2,1,0:T(8,128)S(1)} %get-tuple-element.7.part_ref, bf16[1,1,40,16,128,128]{5,4,3,2,1,0:T(8,128)(2,1)} %w_ref.3), custom_call_target="tpu_custom_call" | custom-call | flops 3019898880 | bytes 20971520 | tf_op jit(solution)/shard_map/exchange/pallas_call | solution.py:397
  27.3 1.2 %deliver.1 = (bf16[1,1,40,144,128]{4,3,2,1,0:T(8,128)(2,1)}, bf16[2,2,144,128]{3,2,1,0:T(8,128)(2,1)}) custom-call(bf16[1,1,40,144,128]{4,3,2,1,0:T(8,128)(2,1)S(1)} %get-tuple-element.8.ocean_ref, bf16[2,2,144,128]{3,2,1,0:T(8,128)(2,1)S(1)} %get-tuple-element.9.part_ref), custom_call_target="tpu_custom_call" | custom-call | tf_op jit(solution)/shard_map/deliver/pallas_call | solution.py:418
Async XLA Ops:
  0.6 8.5 %copy-start = (bf16[2,2,144,128]{3,2,1,0:T(8,128)(2,1)S(1)}, bf16[2,2,144,128]{3,2,1,0:T(8,128)(2,1)}, u32[]{:S(2)}) copy-start(bf16[2,2,144,128]{3,2,1,0:T(8,128)(2,1)} %own_ref.1) | copy-start | bytes 442372
